TPU v7x, 8 devices: a whole 2x2x1 slice. The times are simulated.
8 devices in a mesh: dp: 2 (over z, y), ep: 4 (over x, core).
Axes of the slice: x: 2, y: 2, z: 1, core: 2. Of those that a mesh axis runs over, the one named last changes fastest.
Arguments:
- dispatched: bfloat16 [8, 32, 64, 1024], P('dp', 'ep'), parts along dimension 0
- w_gate: bfloat16 [32, 1024, 512], P('ep')
- w_up: bfloat16 [32, 1024, 512], P('ep')
- w_down: bfloat16 [32, 512, 1024], P('ep')
- fill_count: int32 [8, 32], P('dp', 'ep'), parts along dimension 0
- slot_index: int32 [1024, 8], P(('dp', 'ep')), parts along dimension 0
- expert_id: int32 [1024, 8], P(('dp', 'ep')), parts along dimension 0
- gate_weight: float32 [1024, 8], P(('dp', 'ep')), parts along dimension 0
Outputs:
- output: bfloat16 [1024, 1024], P(('dp', 'ep')), parts along dimension 0
There are 2 independent parts. A program takes and returns all parts, laid end to end along the dimension named above; an argument that names none is the same for every part.
All inputs are finite; a program needn't handle non-finite values.
Results may differ from a plain program's by a relative error of at most 0.001.
Values are sent between devices in bfloat16 or wider.
A program may use at most 1 GiB of HBM per device.

v0:
```python
import jax
import jax.numpy as jnp
from jax import lax
from jax.sharding import PartitionSpec as P


def expert_rows(dispatched, w_gate, w_up, w_down, fill_count):
    capacity = dispatched.shape[2]
    pre_gate = jnp.einsum("secd,edf->escf", dispatched, w_gate, preferred_element_type=jnp.float32)
    pre_up = jnp.einsum("secd,edf->escf", dispatched, w_up, preferred_element_type=jnp.float32)
    hidden = (jax.nn.silu(pre_gate) * pre_up).astype(jnp.bfloat16)
    result = jnp.einsum("escf,efd->escd", hidden, w_down, preferred_element_type=jnp.float32).astype(jnp.bfloat16)
    live_mask = jnp.arange(capacity)[None, None, :] < fill_count.T[:, :, None]
    return jnp.where(live_mask[..., None], result, 0)


def solution(mesh):
    def local_step(dispatched, w_gate, w_up, w_down, fill_count, slot_index, expert_id, gate_weight):
        result = expert_rows(dispatched, w_gate, w_up, w_down, fill_count)
        returned = lax.all_to_all(result, "ep", 1, 0, tiled=True)
        flat_rows = returned.reshape(-1, returned.shape[-1])
        row_index = expert_id * dispatched.shape[2] + jnp.maximum(slot_index, 0)
        picked = jnp.take(flat_rows, row_index, axis=0)
        weight = jnp.where(slot_index >= 0, gate_weight, 0.0)
        combined = jnp.sum(weight[:, :, None] * picked.astype(jnp.float32), axis=1)
        return combined.astype(jnp.bfloat16)
    token_spec = P(("dp", "ep"))
    in_specs = (P("dp", "ep"), P("ep"), P("ep"), P("ep"), P("dp", "ep"), token_spec, token_spec, token_spec)
    return jax.shard_map(local_step, mesh=mesh, in_specs=in_specs, out_specs=token_spec, check_vma=False)
```

profile of v0, /device:TPU:1, one launch (start us, length us, event | category | flops | bytes accessed | tf_op | source)
XLA Modules:
  0.0 89.4 jit_solution(4389450090247935917)
XLA Ops:
  0.0 0.8 copy.21
  0.8 0.1 iota_compare_fusion
  0.8 9.0 %fusion.2 = f32[8,4,64,512]{3,2,1,0:T(8,128)} fusion(bf16[8,1024,512]{2,1,0:T(8,128)(2,1)} %param.10, bf16[4,8,64,1024]{3,2,1,0:T(8,128)(2,1)} %param.8), kind=kOutput, calls=%fused_computation.3 | convolution fusion | flops 2147483648 | bytes 16777216 | tf_op jit(solution)/shard_map/secd,edf->escf/dot_general | solution.py:10
  9.8 12.3 %convert_select_fusion = bf16[8,4,64,1024]{3,2,1,0:T(8,128)(2,1)} fusion(pred[8,4,64]{2,1,0:T(4,128)(4,1)S(1)} %iota_compare_fusion, bf16[8,512,1024]{2,1,0:T(8,128)(2,1)} %param.11, f32[8,4,64,512]{3,2,1,0:T(8,128)} %fusion.2, bf16[8,1024,512]{2,1,0:T(8,128)(2,1)} %param.9, bf16[4,8,64,1024]{3,2,1,0:T(8,128)(2,1)} %param.8), kind=kOutput, calls=%fused_computation.8 | convolution fusion | flops 4305453056 | bytes 29362176 | tf_op jit(solution)/shard_map/escf,efd->escd/dot_general | solution.py:12
  22.1 4.9 %copy.24 = bf16[8,4,64,1024]{3,2,0,1:T(8,128)(2,1)} copy(bf16[8,4,64,1024]{3,2,1,0:T(8,128)(2,1)} %convert_select_fusion) | data formatting | bytes 8388608 | tf_op jit(solution)/shard_map/jit(_where)/select_n | solution.py:14
  27.0 0.0 copy-start
  27.0 0.0 copy-start.2
  27.0 0.0 copy-start.1
  27.0 5.0 %all-to-all-start = ((bf16[8,4,64,1024]{3,2,0,1:T(8,128)(2,1)}), bf16[8,4,64,1024]{3,2,0,1:T(8,128)(2,1)}, u32[]{:S(2)}, u32[]{:S(2)}) async-start(bf16[8,4,64,1024]{3,2,0,1:T(8,128)(2,1)} %copy.24), calls=%async_computation | async-start | bytes 8388608 | tf_op jit(solution)/shard_map/all_to_all | solution.py:20
  32.0 0.0 copy-done
  32.0 0.0 copy-done.2
  32.1 0.1 copy.25
  32.2 0.1 reshape.18
  32.3 0.0 copy-done.1
  32.3 0.1 copy.19
  32.4 0.1 copy.20
  32.5 46.9 %all-to-all-done = bf16[8,4,64,1024]{3,2,0,1:T(8,128)(2,1)} async-done(((bf16[8,4,64,1024]{3,2,0,1:T(8,128)(2,1)}), bf16[8,4,64,1024]{3,2,0,1:T(8,128)(2,1)}, u32[]{:S(2)}, u32[]{:S(2)}) %all-to-all-start) | async-done | bytes 4194336 | tf_op jit(solution)/shard_map/all_to_all | solution.py:20
  79.4 7.7 %gather_fusion = bf16[1024,1024]{1,0:T(8,128)(2,1)S(1)} fusion(bf16[2048,1024]{1,0:T(8,128)(2,1)} %bitcast.9, s32[1024]{0:T(1024)S(1)} %broadcast_clamp_fusion), kind=kCustom, calls=%fused_computation | custom fusion | bytes 4198400 | tf_op jit(solution)/shard_map/jit(_take)/gather | solution.py:23
  87.1 2.2 %multiply_reduce_fusion = bf16[128,1024]{1,0:T(8,128)(2,1)} fusion(bf16[1024,1024]{1,0:T(8,128)(2,1)S(1)} %gather_fusion, f32[128,8]{1,0:T(8,128)S(1)} %copy.19, pred[128,8]{1,0:T(8,128)(4,1)S(1)} %copy.20), kind=kLoop, calls=%fused_computation.7 | loop fusion | flops 4063232 | bytes 2364416 | tf_op jit(solution)/shard_map/reduce_sum | solution.py:25
  (3 shorter events, 0.0 us)
Async XLA Ops:
  27.0 5.0 %copy-start = (s32[128,8]{0,1:T(8,128)S(1)}, s32[128,8]{0,1:T(8,128)}, u32[]{:S(2)}) copy-start(s32[128,8]{0,1:T(8,128)} %param.13) | copy-start | bytes 12292
  27.0 5.0 %copy-start.2 = (s32[128,8]{0,1:T(8,128)S(1)}, s32[128,8]{0,1:T(8,128)}, u32[]{:S(2)}) copy-start(s32[128,8]{0,1:T(8,128)} %param.14) | copy-start | bytes 12292
  27.0 5.2 %copy-start.1 = (f32[128,8]{0,1:T(8,128)S(1)}, f32[128,8]{0,1:T(8,128)}, u32[]{:S(2)}) copy-start(f32[128,8]{0,1:T(8,128)} %param.15) | copy-start | bytes 12292
  27.0 52.4 %all-to-all-start = ((bf16[8,4,64,1024]{3,2,0,1:T(8,128)(2,1)}), bf16[8,4,64,1024]{3,2,0,1:T(8,128)(2,1)}, u32[]{:S(2)}, u32[]{:S(2)}) async-start(bf16[8,4,64,1024]{3,2,0,1:T(8,128)(2,1)} %copy.24), calls=%async_computation | async-start | bytes 8388608 | tf_op jit(solution)/shard_map/all_to_all | solution.py:20
where the time goes:
time: 91.2 us; the launch traced here: 89.4 us
  waiting for transfers between devices  46.9 us (51%)
  matrix products  21.3 us (23%)
  local copies, waits for them, and re-layouts  13.8 us (15%)
  starting transfers between devices  5 us (5%)
  other arithmetic  2.35 us (3%)
    all_to_all x1, waiting for transfers between devices, local_step(): returned = lax.all_to_all(result, 'ep', 1, 0, tiled=True)  46.9 us
    dot_general x1, matrix products, expert_rows(): jnp.einsum('escf,efd->escd', hidden, w_down, preferred_element_type=jnp.f...  12.3 us
    dot_general x1, matrix products, expert_rows(): jnp.einsum('secd,edf->escf', dispatched, w_up, preferred_element_type=jnp...  8.97 us
    gather x1, local copies, waits for them, and re-layouts, local_step(): picked = jnp.take(flat_rows, row_index, axis=0)  7.7 us
    all_to_all x1, starting transfers between devices, local_step(): returned = lax.all_to_all(result, 'ep', 1, 0, tiled=True)  5 us
    select_n x1, local copies, waits for them, and re-layouts, expert_rows(): return jnp.where(live_mask[..., None], result, 0)  4.87 us
    reduce_sum x1, other arithmetic, local_step(): combined = jnp.sum(weight[:, :, None] * picked.astype(jnp.float32), axis=1)  2.25 us
  transfers between devices with their start and end apart: 1, of which 1 were waited for; matrix products, arithmetic and copies ran while one was open for 0% of the time, Pallas kernels for 0%

commit v1 on v0

v1 whole, which is shorter than its diff:
```python
import functools

import jax
import jax.numpy as jnp
from jax import lax
from jax.experimental import pallas as pl
from jax.experimental.pallas import tpu as pltpu
from jax.sharding import PartitionSpec as P

MESH = pl.DeviceIdType.MESH
LOOKAHEAD = 3
CHUNK = 256
BF16_MAX = 3.3895313892515355e38


def split3(value):
    high = jnp.minimum(value, BF16_MAX).astype(jnp.bfloat16)
    rest = value - high.astype(jnp.float32)
    middle = rest.astype(jnp.bfloat16)
    low = (rest - middle.astype(jnp.float32)).astype(jnp.bfloat16)
    return jnp.concatenate([high, middle, low], axis=0)


def kernel(x_hbm, wg_hbm, wu_hbm, wd_hbm, fill_hbm, slot_hbm, expert_hbm, gate_hbm, out_hbm,
           x_buf, wg_buf, wu_buf, wd_buf, fill_buf, slot_buf, expert_buf, gate_buf,
           route_out, route_in, mix, hid, rows_buf, give_buf, keep_buf, from_peer, link_out, link_in, out_buf,
           x_sem, wg_sem, wu_sem, wd_sem, small_sem, out_sem,
           route_send, route_recv, give_send, give_recv, link_send, link_recv):
    experts, width, ffn = wg_hbm.shape
    capacity = x_hbm.shape[2]
    tokens = slot_hbm.shape[1]
    choices = slot_hbm.shape[0]
    chunks = width // CHUNK
    group = lax.axis_index("dp")
    me = lax.axis_index("ep")
    core = lax.rem(me, 2)
    chip = me // 2
    partner = chip * 2 + (1 - core)
    far = (1 - chip) * 2 + core
    far_other = (1 - chip) * 2 + (1 - core)
    sources = (far_other, far, partner, me)

    def x_copy(role, e):
        return pltpu.make_async_copy(
            x_hbm.at[sources[role], e], x_buf.at[e, pl.ds(role * capacity, capacity)], x_sem.at[role, e])

    def wg_copy(e):
        return pltpu.make_async_copy(wg_hbm.at[e], wg_buf.at[e], wg_sem.at[e])

    def wu_copy(e):
        return pltpu.make_async_copy(wu_hbm.at[e], wu_buf.at[e], wu_sem.at[e])

    def wd_copy(n):
        cols = pl.ds(pl.multiple_of(n * CHUNK, CHUNK), CHUNK)
        return pltpu.make_async_copy(wd_hbm.at[:, :, cols], wd_buf.at[:, :, cols], wd_sem.at[n])

    def start_expert(e):
        x_copy(0, e).start()
        x_copy(1, e).start()
        wg_copy(e).start()
        wu_copy(e).start()

    small = [pltpu.make_async_copy(src, dst, small_sem.at[i]) for i, (src, dst) in enumerate(
        ((slot_hbm, slot_buf), (expert_hbm, expert_buf), (gate_hbm, gate_buf), (fill_hbm, fill_buf)))]
    for copy in small:
        copy.start()
    for e in range(LOOKAHEAD):
        start_expert(e)

    barrier = pltpu.get_barrier_semaphore()
    for peer in (partner, far, far_other):
        pl.semaphore_signal(barrier, inc=1, device_id=(group, peer), device_id_type=MESH)

    for copy in small:
        copy.wait()
    slot = slot_buf[...]
    code = jnp.where(slot >= 0, expert_buf[...] * capacity + slot, -1)
    route_out[0:choices] = code.astype(jnp.float32)
    route_out[choices:] = gate_buf[...]

    pl.semaphore_wait(barrier, 3)
    route_copies = [
        pltpu.make_async_remote_copy(
            src_ref=route_out, dst_ref=route_in.at[role], send_sem=route_send.at[role],
            recv_sem=route_recv.at[role], device_id=(group, peer), device_id_type=MESH)
        for role, peer in ((0, far_other), (1, far), (2, partner))]
    for copy in route_copies:
        copy.start()

    def hidden(first, e):
        rows = x_buf[e, pl.ds(first * capacity, 2 * capacity)]
        pre_gate = jnp.dot(rows, wg_buf[e], preferred_element_type=jnp.float32)
        pre_up = jnp.dot(rows, wu_buf[e], preferred_element_type=jnp.float32)
        value = jax.nn.silu(pre_gate) * pre_up
        row = lax.broadcasted_iota(jnp.int32, value.shape, 0)
        limit = jnp.where(row < capacity, fill_buf[sources[first], e], fill_buf[sources[first + 1], e] + capacity)
        hid[e, pl.ds(first * capacity, 2 * capacity)] = jnp.where(row < limit, value, 0.0).astype(jnp.bfloat16)

    def remote_step(e, carry):
        wg_copy(e).wait()
        wu_copy(e).wait()
        x_copy(0, e).wait()
        x_copy(1, e).wait()

        @pl.when(e + LOOKAHEAD < experts)
        def _():
            start_expert(e + LOOKAHEAD)

        @pl.when(e + LOOKAHEAD >= experts)
        def _():
            wd_copy(e + LOOKAHEAD - experts).start()

        hidden(0, e)
        return carry

    lax.fori_loop(0, experts, remote_step, 0)
    for n in range(LOOKAHEAD, chunks):
        wd_copy(n).start()
    for role in (2, 3):
        for e in range(experts):
            x_copy(role, e).start()

    def build_mix(role):
        route = route_out if role == 3 else route_in.at[role]
        code = route[0:choices].astype(jnp.int32)
        gate = route[choices:]
        row = lax.broadcasted_iota(jnp.int32, (experts * capacity, tokens), 0) + me * (experts * capacity)
        value = jnp.zeros((experts * capacity, tokens), jnp.float32)
        for j in range(choices):
            value = jnp.where(row == code[j:j + 1], gate[j:j + 1], value)
        mix[role] = split3(value.T)

    def rows_of(first, n):
        cols = pl.ds(n * CHUNK, CHUNK)
        for e in range(experts):
            value = jnp.dot(hid[e, pl.ds(first * capacity, 2 * capacity)], wd_buf[e, :, cols],
                            preferred_element_type=jnp.float32).astype(jnp.bfloat16)
            rows_buf[0, pl.ds(e * capacity, capacity)] = value[:capacity]
            rows_buf[1, pl.ds(e * capacity, capacity)] = value[capacity:]

    def mixed(role):
        value = jnp.dot(mix[role], rows_buf[role % 2], preferred_element_type=jnp.float32)
        return value[:tokens] + value[tokens:2 * tokens] + value[2 * tokens:]

    def give_copy(kind, n):
        return pltpu.make_async_remote_copy(
            src_ref=give_buf.at[kind, n], dst_ref=from_peer.at[kind, n], send_sem=give_send.at[kind, n],
            recv_sem=give_recv.at[kind, n], device_id=(group, partner), device_id_type=MESH)

    def link_copy(n):
        return pltpu.make_async_remote_copy(
            src_ref=link_out.at[n], dst_ref=link_in.at[n], send_sem=link_send.at[n],
            recv_sem=link_recv.at[n], device_id=(group, far), device_id_type=MESH)

    def send_on(n):
        give_copy(0, n).wait_recv()
        link_out[n] = keep_buf[0, n] + from_peer[0, n]
        link_copy(n).start()

    for role in (0, 1):
        route_copies[role].wait_recv()
        build_mix(role)
    for n in range(chunks):
        wd_copy(n).wait()
        rows_of(0, n)
        give_buf[0, n] = mixed(0)
        give_copy(0, n).start()
        keep_buf[0, n] = mixed(1)
        if n >= 1:
            send_on(n - 1)

    def local_step(e, carry):
        x_copy(2, e).wait()
        x_copy(3, e).wait()
        hidden(2, e)
        return carry

    lax.fori_loop(0, 2, local_step, 0)
    send_on(chunks - 1)
    lax.fori_loop(2, experts, local_step, 0)
    route_copies[2].wait_recv()
    for role in (2, 3):
        build_mix(role)
    for n in range(chunks):
        rows_of(2, n)
        give_buf[1, n] = mixed(2)
        give_copy(1, n).start()
        keep_buf[1, n] = mixed(3)

    for n in range(chunks):
        give_copy(1, n).wait_recv()
        near = keep_buf[1, n] + from_peer[1, n]
        link_copy(n).wait_recv()
        cols = pl.ds(n * CHUNK, CHUNK)
        out_buf[:, cols] = (near + link_in[n]).astype(jnp.bfloat16)
        pltpu.make_async_copy(out_buf.at[:, cols], out_hbm.at[:, cols], out_sem.at[n]).start()
    for n in range(chunks):
        cols = pl.ds(n * CHUNK, CHUNK)
        pltpu.make_async_copy(out_buf.at[:, cols], out_hbm.at[:, cols], out_sem.at[n]).wait()
        for kind in range(2):
            give_copy(kind, n).wait_send()
        link_copy(n).wait_send()
    for copy in route_copies:
        copy.wait_send()


def solution(mesh):
    def local_step(dispatched, w_gate, w_up, w_down, fill_count, slot_index, expert_id, gate_weight):
        sources, experts, capacity, width = dispatched.shape
        ffn = w_gate.shape[2]
        tokens, choices = slot_index.shape
        chunks = width // CHUNK
        f32, bf16 = jnp.float32, jnp.bfloat16
        any_spec = pl.BlockSpec(memory_space=pl.ANY)
        scratch = [
            pltpu.VMEM((experts, sources * capacity, width), bf16),
            pltpu.VMEM((experts, width, ffn), bf16),
            pltpu.VMEM((experts, width, ffn), bf16),
            pltpu.VMEM((experts, ffn, width), bf16),
            pltpu.SMEM((sources, experts), jnp.int32),
            pltpu.VMEM((choices, tokens), jnp.int32),
            pltpu.VMEM((choices, tokens), jnp.int32),
            pltpu.VMEM((choices, tokens), f32),
            pltpu.VMEM((2 * choices, tokens), f32),
            pltpu.VMEM((3, 2 * choices, tokens), f32),
            pltpu.VMEM((4, 3 * tokens, experts * capacity), bf16),
            pltpu.VMEM((experts, sources * capacity, ffn), bf16),
            pltpu.VMEM((2, experts * capacity, CHUNK), bf16),
            pltpu.VMEM((2, chunks, tokens, CHUNK), f32),
            pltpu.VMEM((2, chunks, tokens, CHUNK), f32),
            pltpu.VMEM((2, chunks, tokens, CHUNK), f32),
            pltpu.VMEM((chunks, tokens, CHUNK), f32),
            pltpu.VMEM((chunks, tokens, CHUNK), f32),
            pltpu.VMEM((tokens, width), bf16),
            pltpu.SemaphoreType.DMA((4, experts)),
            pltpu.SemaphoreType.DMA((experts,)),
            pltpu.SemaphoreType.DMA((experts,)),
            pltpu.SemaphoreType.DMA((chunks,)),
            pltpu.SemaphoreType.DMA((4,)),
            pltpu.SemaphoreType.DMA((chunks,)),
            pltpu.SemaphoreType.DMA((3,)),
            pltpu.SemaphoreType.DMA((3,)),
            pltpu.SemaphoreType.DMA((2, chunks)),
            pltpu.SemaphoreType.DMA((2, chunks)),
            pltpu.SemaphoreType.DMA((chunks,)),
            pltpu.SemaphoreType.DMA((chunks,)),
        ]
        return pl.pallas_call(
            kernel,
            out_shape=jax.ShapeDtypeStruct((tokens, width), bf16),
            in_specs=[any_spec] * 8,
            out_specs=any_spec,
            scratch_shapes=scratch,
            compiler_params=pltpu.CompilerParams(
                collective_id=0, has_side_effects=True, vmem_limit_bytes=60 * 1024 * 1024),
            name="expert_return",
        )(dispatched, w_gate, w_up, w_down, fill_count, slot_index.T, expert_id.T, gate_weight.T)

    token_spec = P(("dp", "ep"))
    in_specs = (P("dp", "ep"), P("ep"), P("ep"), P("ep"), P("dp", "ep"), token_spec, token_spec, token_spec)
    return jax.shard_map(local_step, mesh=mesh, in_specs=in_specs, out_specs=token_spec, check_vma=False)
```

time: 91.2 us -> 28.4 us (0.31)
  the two profiles are of different devices: /device:TPU:1 before, /device:TPU:0 now
where the time goes in v1:
time: 28.4 us; the launch traced here: 28.3 us
  Pallas kernels  26.6 us (94%)
  local copies, waits for them, and re-layouts  1.67 us (6%)
    pallas_call x1, Pallas kernels, local_step(): pl.pallas_call(kernel, out_shape=jax.ShapeDtypeStruct((tokens, width), bf...  26.6 us
    unnamed x1, local copies, waits for them, and re-layouts  1.67 us

profile of v1, /device:TPU:0, one launch (start us, length us, event | category | flops | bytes accessed | tf_op | source)
XLA Modules:
  0.0 28.3 jit_solution(10714298597470885605)
XLA Ops:
  0.0 26.6 %expert_return.1 = bf16[128,1024]{1,0:T(8,128)(2,1)} custom-call(bf16[4,8,64,1024]{3,2,1,0:T(8,128)(2,1)} %x_hbm.1, bf16[8,1024,512]{2,1,0:T(8,128)(2,1)} %wg_hbm.1, bf16[8,1024,512]{2,1,0:T(8,128)(2,1)} %wu_hbm.1, bf16[8,512,1024]{2,1,0:T(8,128)(2,1)} %wd_hbm.1, s32[4,8]{1,0:T(4,128)} %fill_hbm.1, s32[8,128]{1,0:T(8,128)} %bitcast.3, s32[8,128]{1,0:T(8,128)} %bitcast.4, ...), custom_call_target="tpu_custom_call" | custom-call | tf_op jit(solution)/shard_map/expert_return/pallas_call | solution.py:248
  26.6 1.7 %copy.10 = bf16[128,1024]{1,0:T(8,128)(2,1)} copy(bf16[128,1024]{1,0:T(8,128)(2,1)} %expert_return.1) | data formatting | bytes 524288

commit v2 on v0

v2 whole, which is shorter than its diff:
```python
import jax
import jax.numpy as jnp
from jax import lax
from jax.experimental import pallas as pl
from jax.experimental.pallas import tpu as pltpu
from jax.sharding import PartitionSpec as P

MESH = pl.DeviceIdType.MESH
RING = 3
CHUNK = 256
DIRECT = 48
BF16_MAX = 3.3895313892515355e38


def split3(value):
    high = jnp.minimum(value, BF16_MAX).astype(jnp.bfloat16)
    rest = value - high.astype(jnp.float32)
    middle = rest.astype(jnp.bfloat16)
    low = (rest - middle.astype(jnp.float32)).astype(jnp.bfloat16)
    return jnp.concatenate([high, middle, low], axis=0)


def kernel(x_hbm, wg_hbm, wu_hbm, wd_hbm, fill_hbm, slot_hbm, expert_hbm, gate_hbm, out_ref,
           x_buf, w_buf, wd_buf, fill_buf, id_buf, gate_buf,
           route_out, route_in, mix, hid, rows_buf, sums, from_peer, link_out, link_in, direct_in,
           w_sem, x_sem, small_sem, route_send, route_recv, give_send, give_recv, link_send, link_recv,
           direct_send, rest_send, side_recv):
    experts = wg_hbm.shape[0]
    capacity, width = x_hbm.shape[2:]
    choices, tokens = slot_hbm.shape
    chunks = width // CHUNK
    pair = 2 * capacity
    half = experts // 2
    group = lax.axis_index("dp")
    me = lax.axis_index("ep")
    core = lax.rem(me, 2)
    chip = me // 2
    partner = chip * 2 + (1 - core)
    far = (1 - chip) * 2 + core
    far_other = (1 - chip) * 2 + (1 - core)
    sources = (far_other, far, partner, me)

    def start_expert(e):
        for role in range(2):
            pltpu.make_async_copy(
                x_hbm.at[sources[role], e], x_buf.at[e, pl.ds(role * capacity, capacity)],
                x_sem.at[lax.rem(e, RING)]).start()
        for i, src in enumerate((wg_hbm, wu_hbm)):
            pltpu.make_async_copy(src.at[e], w_buf.at[e, i], w_sem.at[lax.rem(e, RING)]).start()

    def start_step(e, carry):
        start_expert(e)
        return carry

    def early_down_copy(e):
        return pltpu.make_async_copy(
            wd_hbm.at[e, :, pl.ds(0, CHUNK)], wd_buf.at[e, :, pl.ds(0, CHUNK)], x_sem.at[lax.rem(e + half, RING)])

    def wait_expert(e, late):
        part = x_buf.at[e] if late else x_buf.at[e, pl.ds(0, pair)]
        pltpu.make_async_copy(part, part, x_sem.at[lax.rem(e, RING)]).wait()
        pltpu.make_async_copy(w_buf.at[e], w_buf.at[e], w_sem.at[lax.rem(e, RING)]).wait()

    def down_copy(n):
        some = pl.ds(half, half) if n == 0 else pl.ds(0, experts)
        cols = pl.ds(n * CHUNK, CHUNK)
        return pltpu.make_async_copy(
            wd_hbm.at[some, :, cols], wd_buf.at[some, :, cols], w_sem.at[(experts + n) % RING])

    small = [pltpu.make_async_copy(src, dst, small_sem.at[i]) for i, (src, dst) in enumerate(
        ((slot_hbm, id_buf.at[0]), (expert_hbm, id_buf.at[1]), (gate_hbm, gate_buf), (fill_hbm, fill_buf)))]
    for copy in small:
        copy.start()
    lax.fori_loop(0, RING, start_step, 0)

    barrier = pltpu.get_barrier_semaphore()
    for peer in (partner, far, far_other):
        pl.semaphore_signal(barrier, inc=1, device_id=(group, peer), device_id_type=MESH)

    for copy in small:
        copy.wait()
    slot = id_buf[0]
    code = jnp.where(slot >= 0, id_buf[1] * capacity + slot, -1)
    route_out[0:choices] = code.astype(jnp.float32)
    route_out[choices:] = gate_buf[...]

    with jax.named_scope("bar"):
        pl.semaphore_wait(barrier, 3)
    for role, peer in ((0, far_other), (1, far), (2, partner)):
        pltpu.make_async_remote_copy(
            src_ref=route_out, dst_ref=route_in.at[role], send_sem=route_send, recv_sem=route_recv,
            device_id=(group, peer), device_id_type=MESH).start()

    def route_all(src, dst):
        return pltpu.make_async_remote_copy(
            src_ref=route_in, dst_ref=route_in, send_sem=route_send, recv_sem=route_recv,
            device_id=(group, partner), device_id_type=MESH)

    def hidden(first, e):
        rows = x_buf[e, pl.ds(first * capacity, pair)]
        pre_gate = jnp.dot(rows, w_buf[e, 0], preferred_element_type=jnp.float32)
        pre_up = jnp.dot(rows, w_buf[e, 1], preferred_element_type=jnp.float32)
        value = jax.nn.silu(pre_gate) * pre_up
        row = lax.broadcasted_iota(jnp.int32, value.shape, 0)
        limit = jnp.where(row < capacity, fill_buf[sources[first], e], fill_buf[sources[first + 1], e] + capacity)
        hid[e, pl.ds(first * capacity, pair)] = jnp.where(row < limit, value, 0.0).astype(jnp.bfloat16)

    def first_step(e, carry):
        with jax.named_scope("w_e"):
            wait_expert(e, False)

        @pl.when(e + RING >= half)
        def _():
            early_down_copy(e + RING - half).start()

        start_expert(e + RING)
        with jax.named_scope("hid"):
            hidden(0, e)
        return carry

    def late_step(e, carry):
        with jax.named_scope("w_e"):
            wait_expert(e, True)

        @pl.when(e + RING < experts)
        def _():
            early_down_copy(e + RING - half).start()
            start_expert(e + RING)

        for n in range(RING):
            @pl.when(e + RING == experts + n)
            def _():
                down_copy(n).start()

        with jax.named_scope("hid"):
            rows_of(0, 0, e - half)
            hidden(0, e)
        return carry

    def build_mix(role):
        route = route_out if role == 3 else route_in.at[role]
        code = route[0:choices].astype(jnp.int32)
        gate = route[choices:]
        row = lax.broadcasted_iota(jnp.int32, (experts * capacity, tokens), 0) + me * (experts * capacity)
        value = jnp.zeros((experts * capacity, tokens), jnp.float32)
        for j in range(choices):
            value = jnp.where(row == code[j:j + 1], gate[j:j + 1], value)
        value = value.T
        block = tokens // 2
        mix[role, 0:3 * block] = split3(value[:block])
        mix[role, 3 * block:] = split3(value[block:])

    def rows_of(first, n, e):
        value = jnp.dot(hid[e, pl.ds(first * capacity, pair)], wd_buf[e, :, pl.ds(n * CHUNK, CHUNK)],
                        preferred_element_type=jnp.float32).astype(jnp.bfloat16)
        here = pl.ds(e * capacity, capacity)
        rows_buf[0, here] = value[:capacity]
        rows_buf[1, here] = value[capacity:]

    def mixed(role):
        block = tokens // 2
        parts = []
        for part in range(2):
            value = jnp.dot(mix[role, pl.ds(part * 3 * block, 3 * block)], rows_buf[role % 2],
                            preferred_element_type=jnp.float32)
            parts.append(value[:block] + value[block:2 * block] + value[2 * block:])
        return jnp.concatenate(parts, axis=0)

    def give_copy(kind, n):
        return pltpu.make_async_remote_copy(
            src_ref=sums.at[kind, 0, n], dst_ref=from_peer.at[kind, n], send_sem=give_send,
            recv_sem=give_recv.at[n if kind == 0 else chunks], device_id=(group, partner), device_id_type=MESH)

    direct_copy = pltpu.make_async_remote_copy(
        src_ref=sums.at[0, 1 - core, 0, pl.ds(0, DIRECT)], dst_ref=direct_in.at[core], send_sem=direct_send,
        recv_sem=side_recv, device_id=(group, (1 - chip) * 2), device_id_type=MESH)
    rest_copy = pltpu.make_async_remote_copy(
        src_ref=link_out.at[0, pl.ds(0, DIRECT)], dst_ref=link_in.at[0, pl.ds(0, DIRECT)], send_sem=rest_send,
        recv_sem=side_recv, device_id=(group, far), device_id_type=MESH)

    def link_copy(n):
        part = pl.ds(DIRECT, tokens - DIRECT) if n == 0 else pl.ds(0, tokens)
        return pltpu.make_async_remote_copy(
            src_ref=link_out.at[n, part], dst_ref=link_in.at[n, part], send_sem=link_send,
            recv_sem=link_recv.at[n], device_id=(group, far), device_id_type=MESH)

    def send_on(n):
        give_copy(0, n).wait_recv()
        link_out[n] = sums[0, 1, n] + from_peer[0, n]
        if n == 0:
            @pl.when(core == 1)
            def _():
                rest_copy.start()
        link_copy(n).start()

    lax.fori_loop(0, half, first_step, 0)
    with jax.named_scope("w_route"):
        route_all(0, 0).wait_recv()
    with jax.named_scope("mix"):
        build_mix(0)
    lax.fori_loop(half, half + 2, late_step, 0)
    with jax.named_scope("mix"):
        build_mix(1)
    lax.fori_loop(half + 2, experts, late_step, 0)

    for n in range(chunks):
        with jax.named_scope("w_d"):
            down_copy(n).wait()
        if n + RING < chunks:
            down_copy(n + RING).start()
        if n == 0:
            for role in (2, 3):
                pltpu.make_async_copy(
                    x_hbm.at[sources[role]], x_buf.at[:, pl.ds(role * capacity, capacity)], small_sem.at[0]).start()
        with jax.named_scope("rows"):
            for e in range(half if n == 0 else 0, experts):
                rows_of(0, n, e)
        with jax.named_scope("mixed"):
            sums[0, 0, n] = mixed(0)
            if n == 0:
                give_copy(0, n).start()

                @pl.when(core == 1)
                def _():
                    direct_copy.start()
            sums[0, 1, n] = mixed(1)
            if n == 0:
                @pl.when(core == 0)
                def _():
                    direct_copy.start()
            else:
                give_copy(0, n).start()
        with jax.named_scope("send_on"):
            if n == 0:
                send_on(n)
            if n >= 2:
                send_on(n - 1)

    local_rows = x_buf.at[:, pl.ds(pair, pair)]
    pltpu.make_async_copy(local_rows, local_rows, small_sem.at[0]).wait()

    def local_step(e, carry):
        hidden(2, e)
        return carry

    lax.fori_loop(0, 2, local_step, 0)
    send_on(chunks - 1)
    with jax.named_scope("phase1L"):
        lax.fori_loop(2, experts, local_step, 0)
    for role in (2, 3):
        build_mix(role)
    for n in range(chunks):
        with jax.named_scope("rows2"):
            for e in range(experts):
                rows_of(2, n, e)
        with jax.named_scope("mixed2"):
            sums[1, 0, n] = mixed(2)
            sums[1, 1, n] = mixed(3)
            give_copy(1, n).start()

    with jax.named_scope("fin_give"):
        pltpu.make_async_remote_copy(
            src_ref=sums.at[1, 0], dst_ref=from_peer.at[1], send_sem=give_send, recv_sem=give_recv.at[chunks],
            device_id=(group, partner), device_id_type=MESH).wait_recv()

    with jax.named_scope("fin_side"):
        @pl.when(core == 0)
        def _():
            pltpu.make_async_remote_copy(
                src_ref=direct_in, dst_ref=direct_in, send_sem=direct_send, recv_sem=side_recv,
                device_id=(group, far), device_id_type=MESH).wait_recv()
            link_in[0, 0:DIRECT] = direct_in[0] + direct_in[1]

        @pl.when(core == 1)
        def _():
            rest_copy.wait_recv()

    for n in range(chunks):
        near = sums[1, 1, n] + from_peer[1, n]
        with jax.named_scope("fin_link"):
            link_copy(n).wait_recv()
        out_ref[:, pl.ds(n * CHUNK, CHUNK)] = (near + link_in[n]).astype(jnp.bfloat16)

    with jax.named_scope("w_send"):
        all_given = sums.at[:, 0]
        pltpu.make_async_remote_copy(
            src_ref=all_given, dst_ref=from_peer, send_sem=give_send, recv_sem=give_recv.at[chunks],
            device_id=(group, partner), device_id_type=MESH).wait_send()
        sent = link_out.at[pl.ds(0, chunks - 1)]
        first = link_out.at[0, pl.ds(DIRECT, tokens - DIRECT)]
        for part in (sent, first):
            pltpu.make_async_remote_copy(
                src_ref=part, dst_ref=part, send_sem=link_send, recv_sem=link_recv.at[0],
                device_id=(group, far), device_id_type=MESH).wait_send()
        direct_copy.wait_send()

        @pl.when(core == 1)
        def _():
            rest_copy.wait_send()
        route_all(0, 0).wait_send()


def solution(mesh):
    def local_step(dispatched, w_gate, w_up, w_down, fill_count, slot_index, expert_id, gate_weight):
        sources, experts, capacity, width = dispatched.shape
        ffn = w_gate.shape[2]
        tokens, choices = slot_index.shape
        chunks = width // CHUNK
        f32, bf16 = jnp.float32, jnp.bfloat16
        scratch = [
            pltpu.VMEM((experts, sources * capacity, width), bf16),
            pltpu.VMEM((experts, 2, width, ffn), bf16),
            pltpu.VMEM((experts, ffn, width), bf16),
            pltpu.SMEM((sources, experts), jnp.int32),
            pltpu.VMEM((2, choices, tokens), jnp.int32),
            pltpu.VMEM((choices, tokens), f32),
            pltpu.VMEM((2 * choices, tokens), f32),
            pltpu.VMEM((3, 2 * choices, tokens), f32),
            pltpu.VMEM((4, 3 * tokens, experts * capacity), bf16),
            pltpu.VMEM((experts, sources * capacity, ffn), bf16),
            pltpu.VMEM((2, experts * capacity, CHUNK), bf16),
            pltpu.VMEM((2, 2, chunks, tokens, CHUNK), f32),
            pltpu.VMEM((2, chunks, tokens, CHUNK), f32),
            pltpu.VMEM((chunks, tokens, CHUNK), f32),
            pltpu.VMEM((chunks, tokens, CHUNK), f32),
            pltpu.VMEM((2, DIRECT, CHUNK), f32),
            pltpu.SemaphoreType.DMA((RING,)),
            pltpu.SemaphoreType.DMA((RING,)),
            pltpu.SemaphoreType.DMA((4,)),
            pltpu.SemaphoreType.DMA,
            pltpu.SemaphoreType.DMA,
            pltpu.SemaphoreType.DMA,
            pltpu.SemaphoreType.DMA((chunks + 1,)),
            pltpu.SemaphoreType.DMA,
            pltpu.SemaphoreType.DMA((chunks,)),
            pltpu.SemaphoreType.DMA,
            pltpu.SemaphoreType.DMA,
            pltpu.SemaphoreType.DMA,
        ]
        operands = (dispatched, w_gate, w_up, w_down, fill_count, slot_index.T, expert_id.T, gate_weight.T)
        return pl.pallas_call(
            kernel,
            out_shape=pltpu.VMEM((tokens, width), bf16),
            in_specs=[pl.BlockSpec(memory_space=pl.ANY)] * len(operands),
            out_specs=pl.BlockSpec(memory_space=pltpu.VMEM),
            scratch_shapes=scratch,
            compiler_params=pltpu.CompilerParams(
                collective_id=0, has_side_effects=True, vmem_limit_bytes=44 * 1024 * 1024),
            name="expert_return",
        )(*(pltpu.with_memory_space_constraint(array, pltpu.HBM) for array in operands))

    token_spec = P(("dp", "ep"))
    in_specs = (P("dp", "ep"), P("ep"), P("ep"), P("ep"), P("dp", "ep"), token_spec, token_spec, token_spec)
    return jax.shard_map(local_step, mesh=mesh, in_specs=in_specs, out_specs=token_spec, check_vma=False)
```

time: 91.2 us -> 25.3 us (0.28)
  the two profiles are of different devices: /device:TPU:1 before, /device:TPU:0 now
where the time goes in v2:
time: 25.3 us; the launch traced here: 25.1 us
  Pallas kernels  24.4 us (96%)
  local copies, waits for them, and re-layouts  0.71 us (3%)
    pallas_call x1, Pallas kernels, local_step(): pl.pallas_call(kernel, out_shape=pltpu.VMEM((tokens, width), bf16), in_sp...  24.4 us
    unnamed x1, local copies, waits for them, and re-layouts  0.71 us

profile of v2, /device:TPU:0, one launch (start us, length us, event | category | flops | bytes accessed | tf_op | source)
XLA Modules:
  0.0 25.1 jit_solution(6269621408192171730)
XLA Ops:
  0.0 24.4 %expert_return.1 = bf16[128,1024]{1,0:T(8,128)(2,1)S(1)} custom-call(bf16[4,8,64,1024]{3,2,1,0:T(8,128)(2,1)} %x_hbm.1, bf16[8,1024,512]{2,1,0:T(8,128)(2,1)} %wg_hbm.1, bf16[8,1024,512]{2,1,0:T(8,128)(2,1)} %wu_hbm.1, bf16[8,512,1024]{2,1,0:T(8,128)(2,1)} %wd_hbm.1, s32[4,8]{1,0:T(4,128)} %fill_hbm.1, s32[8,128]{1,0:T(8,128)} %bitcast.3, s32[8,128]{1,0:T(8,128)} %bitcast.4, ...), custom_call_target="tpu_custom_call" | custom-call | tf_op jit(solution)/shard_map/expert_return/pallas_call | solution.py:341
  24.4 0.7 %copy.10 = bf16[128,1024]{1,0:T(8,128)(2,1)} copy(bf16[128,1024]{1,0:T(8,128)(2,1)S(1)} %expert_return.1) | data formatting | bytes 524288

commit v3 on v2

--- a/solution.py
+++ b/solution.py
@@ -6,9 +6,10 @@
 from jax.sharding import PartitionSpec as P
 
 MESH = pl.DeviceIdType.MESH
-RING = 3
+RING = 4
 CHUNK = 256
-DIRECT = 48
+DIRECT = 64
+LENT = 32
 BF16_MAX = 3.3895313892515355e38
 
 
@@ -22,9 +23,8 @@
 
 def kernel(x_hbm, wg_hbm, wu_hbm, wd_hbm, fill_hbm, slot_hbm, expert_hbm, gate_hbm, out_ref,
            x_buf, w_buf, wd_buf, fill_buf, id_buf, gate_buf,
-           route_out, route_in, mix, hid, rows_buf, sums, from_peer, link_out, link_in, direct_in,
-           w_sem, x_sem, small_sem, route_send, route_recv, give_send, give_recv, link_send, link_recv,
-           direct_send, rest_send, side_recv):
+           route_out, route_in, mix, hid, rows_buf, sums, from_peer, link_out, link_in, side_in, lent_in, lent_out,
+           w_sem, x_sem, small_sem, send_sem, route_recv, give_recv, link_recv, side_recv, lent_recv):
     experts = wg_hbm.shape[0]
     capacity, width = x_hbm.shape[2:]
     choices, tokens = slot_hbm.shape
@@ -45,8 +45,8 @@
             pltpu.make_async_copy(
                 x_hbm.at[sources[role], e], x_buf.at[e, pl.ds(role * capacity, capacity)],
                 x_sem.at[lax.rem(e, RING)]).start()
-        for i, src in enumerate((wg_hbm, wu_hbm)):
-            pltpu.make_async_copy(src.at[e], w_buf.at[e, i], w_sem.at[lax.rem(e, RING)]).start()
+        for which, src in enumerate((wg_hbm, wu_hbm)):
+            pltpu.make_async_copy(src.at[e], w_buf.at[e, which], w_sem.at[lax.rem(e, RING)]).start()
 
     def start_step(e, carry):
         start_expert(e)
@@ -88,12 +88,12 @@
         pl.semaphore_wait(barrier, 3)
     for role, peer in ((0, far_other), (1, far), (2, partner)):
         pltpu.make_async_remote_copy(
-            src_ref=route_out, dst_ref=route_in.at[role], send_sem=route_send, recv_sem=route_recv,
+            src_ref=route_out, dst_ref=route_in.at[role], send_sem=send_sem, recv_sem=route_recv,
             device_id=(group, peer), device_id_type=MESH).start()
 
     def route_all(src, dst):
         return pltpu.make_async_remote_copy(
-            src_ref=route_in, dst_ref=route_in, send_sem=route_send, recv_sem=route_recv,
+            src_ref=route_in, dst_ref=route_in, send_sem=send_sem, recv_sem=route_recv,
             device_id=(group, partner), device_id_type=MESH)
 
     def hidden(first, e):
@@ -161,36 +161,52 @@
         block = tokens // 2
         parts = []
         for part in range(2):
-            value = jnp.dot(mix[role, pl.ds(part * 3 * block, 3 * block)], rows_buf[role % 2],
+            value = jnp.dot(mix[role, pl.ds(part * 3 * block, 3 * block)], rows_buf[lax.rem(role, 2)],
                             preferred_element_type=jnp.float32)
             parts.append(value[:block] + value[block:2 * block] + value[2 * block:])
         return jnp.concatenate(parts, axis=0)
 
     def give_copy(kind, n):
         return pltpu.make_async_remote_copy(
-            src_ref=sums.at[kind, 0, n], dst_ref=from_peer.at[kind, n], send_sem=give_send,
+            src_ref=sums.at[kind, 0, n], dst_ref=from_peer.at[kind, n], send_sem=send_sem,
             recv_sem=give_recv.at[n if kind == 0 else chunks], device_id=(group, partner), device_id_type=MESH)
 
     direct_copy = pltpu.make_async_remote_copy(
-        src_ref=sums.at[0, 1 - core, 0, pl.ds(0, DIRECT)], dst_ref=direct_in.at[core], send_sem=direct_send,
-        recv_sem=side_recv, device_id=(group, (1 - chip) * 2), device_id_type=MESH)
+        src_ref=sums.at[0, 1 - core, 0, pl.ds(0, DIRECT)], dst_ref=side_in.at[pl.ds(core * DIRECT, DIRECT)],
+        send_sem=send_sem, recv_sem=side_recv, device_id=(group, (1 - chip) * 2), device_id_type=MESH)
     rest_copy = pltpu.make_async_remote_copy(
-        src_ref=link_out.at[0, pl.ds(0, DIRECT)], dst_ref=link_in.at[0, pl.ds(0, DIRECT)], send_sem=rest_send,
+        src_ref=link_out.at[0, pl.ds(0, DIRECT)], dst_ref=link_in.at[0, pl.ds(0, DIRECT)], send_sem=send_sem,
         recv_sem=side_recv, device_id=(group, far), device_id_type=MESH)
+    lend_copy = pltpu.make_async_remote_copy(
+        src_ref=sums.at[0, 1, 1, pl.ds(0, LENT)], dst_ref=lent_in, send_sem=send_sem, recv_sem=lent_recv,
+        device_id=(group, partner), device_id_type=MESH)
+    lent_copy = pltpu.make_async_remote_copy(
+        src_ref=lent_out, dst_ref=side_in.at[pl.ds(2 * DIRECT, LENT)], send_sem=send_sem, recv_sem=side_recv,
+        device_id=(group, far_other), device_id_type=MESH)
+    own_copy = pltpu.make_async_remote_copy(
+        src_ref=link_out.at[1, pl.ds(0, LENT)], dst_ref=link_in.at[1, pl.ds(0, LENT)], send_sem=send_sem,
+        recv_sem=side_recv, device_id=(group, far), device_id_type=MESH)
 
     def link_copy(n):
-        part = pl.ds(DIRECT, tokens - DIRECT) if n == 0 else pl.ds(0, tokens)
+        skip = DIRECT if n == 0 else LENT if n == 1 else 0
+        part = pl.ds(skip, tokens - skip)
         return pltpu.make_async_remote_copy(
-            src_ref=link_out.at[n, part], dst_ref=link_in.at[n, part], send_sem=link_send,
+            src_ref=link_out.at[n, part], dst_ref=link_in.at[n, part], send_sem=send_sem,
             recv_sem=link_recv.at[n], device_id=(group, far), device_id_type=MESH)
 
     def send_on(n):
         give_copy(0, n).wait_recv()
-        link_out[n] = sums[0, 1, n] + from_peer[0, n]
-        if n == 0:
+        if n == 1:
             @pl.when(core == 1)
             def _():
-                rest_copy.start()
+                lend_copy.wait_recv()
+                lent_out[...] = sums[0, 0, 1, 0:LENT] + lent_in[...]
+                lent_copy.start()
+        link_out[n] = sums[0, 1, n] + from_peer[0, n]
+        if n <= 1:
+            @pl.when(core == 1)
+            def _():
+                (rest_copy, own_copy)[n].start()
         link_copy(n).start()
 
     lax.fori_loop(0, half, first_step, 0)
@@ -203,38 +219,69 @@
         build_mix(1)
     lax.fori_loop(half + 2, experts, late_step, 0)
 
-    for n in range(chunks):
+    def remote_rows(n, between=lambda: None):
         with jax.named_scope("w_d"):
             down_copy(n).wait()
         if n + RING < chunks:
             down_copy(n + RING).start()
-        if n == 0:
-            for role in (2, 3):
-                pltpu.make_async_copy(
-                    x_hbm.at[sources[role]], x_buf.at[:, pl.ds(role * capacity, capacity)], small_sem.at[0]).start()
         with jax.named_scope("rows"):
-            for e in range(half if n == 0 else 0, experts):
+            for e in range(half, experts):
                 rows_of(0, n, e)
+        between()
+        if n > 0:
+            with jax.named_scope("rows"):
+                for e in range(half):
+                    rows_of(0, n, e)
+
+    def remote_sums(n):
         with jax.named_scope("mixed"):
-            sums[0, 0, n] = mixed(0)
             if n == 0:
-                give_copy(0, n).start()
+                sums[0, 1 - core, 0] = mixed(1 - core)
 
                 @pl.when(core == 1)
                 def _():
-                    direct_copy.start()
-            sums[0, 1, n] = mixed(1)
-            if n == 0:
+                    give_copy(0, 0).start()
+
+                direct_copy.start()
+                sums[0, core, 0] = mixed(core)
+
                 @pl.when(core == 0)
                 def _():
-                    direct_copy.start()
+                    give_copy(0, 0).start()
             else:
+                sums[0, 0, n] = mixed(0)
+                sums[0, 1, n] = mixed(1)
                 give_copy(0, n).start()
+            if n == 1:
+                @pl.when(core == 0)
+                def _():
+                    lend_copy.start()
+
+    remote_rows(0)
+    for role in (2, 3):
+        pltpu.make_async_copy(
+            x_hbm.at[sources[role]], x_buf.at[:, pl.ds(role * capacity, capacity)], small_sem.at[0]).start()
+    remote_sums(0)
+
+    def send_first():
+        @pl.when(core == 0)
+        def _():
+            with jax.named_scope("send_on"):
+                send_on(0)
+
+    remote_rows(1, send_first)
+    remote_sums(1)
+
+    @pl.when(core == 1)
+    def _():
         with jax.named_scope("send_on"):
-            if n == 0:
-                send_on(n)
-            if n >= 2:
-                send_on(n - 1)
+            send_on(0)
+
+    for n in range(2, chunks):
+        remote_rows(n)
+        remote_sums(n)
+        with jax.named_scope("send_on"):
+            send_on(n - 1)
 
     local_rows = x_buf.at[:, pl.ds(pair, pair)]
     pltpu.make_async_copy(local_rows, local_rows, small_sem.at[0]).wait()
@@ -260,20 +307,24 @@
 
     with jax.named_scope("fin_give"):
         pltpu.make_async_remote_copy(
-            src_ref=sums.at[1, 0], dst_ref=from_peer.at[1], send_sem=give_send, recv_sem=give_recv.at[chunks],
+            src_ref=sums.at[1, 0], dst_ref=from_peer.at[1], send_sem=send_sem, recv_sem=give_recv.at[chunks],
             device_id=(group, partner), device_id_type=MESH).wait_recv()
 
     with jax.named_scope("fin_side"):
         @pl.when(core == 0)
         def _():
             pltpu.make_async_remote_copy(
-                src_ref=direct_in, dst_ref=direct_in, send_sem=direct_send, recv_sem=side_recv,
+                src_ref=side_in, dst_ref=side_in, send_sem=send_sem, recv_sem=side_recv,
                 device_id=(group, far), device_id_type=MESH).wait_recv()
-            link_in[0, 0:DIRECT] = direct_in[0] + direct_in[1]
+            link_in[0, 0:DIRECT] = side_in[0:DIRECT] + side_in[DIRECT:2 * DIRECT]
+            link_in[1, 0:LENT] = side_in[2 * DIRECT:]
 
         @pl.when(core == 1)
         def _():
-            rest_copy.wait_recv()
+            both = link_in.at[0, pl.ds(0, DIRECT + LENT)]
+            pltpu.make_async_remote_copy(
+                src_ref=both, dst_ref=both, send_sem=send_sem, recv_sem=side_recv,
+                device_id=(group, far), device_id_type=MESH).wait_recv()
 
     for n in range(chunks):
         near = sums[1, 1, n] + from_peer[1, n]
@@ -282,22 +333,25 @@
         out_ref[:, pl.ds(n * CHUNK, CHUNK)] = (near + link_in[n]).astype(jnp.bfloat16)
 
     with jax.named_scope("w_send"):
-        all_given = sums.at[:, 0]
-        pltpu.make_async_remote_copy(
-            src_ref=all_given, dst_ref=from_peer, send_sem=give_send, recv_sem=give_recv.at[chunks],
-            device_id=(group, partner), device_id_type=MESH).wait_send()
-        sent = link_out.at[pl.ds(0, chunks - 1)]
-        first = link_out.at[0, pl.ds(DIRECT, tokens - DIRECT)]
-        for part in (sent, first):
+        def wait_sent(ref):
             pltpu.make_async_remote_copy(
-                src_ref=part, dst_ref=part, send_sem=link_send, recv_sem=link_recv.at[0],
+                src_ref=ref, dst_ref=ref, send_sem=send_sem, recv_sem=side_recv,
                 device_id=(group, far), device_id_type=MESH).wait_send()
+
+        wait_sent(route_in)
+        wait_sent(from_peer)
+        for n in range(chunks):
+            link_copy(n).wait_send()
         direct_copy.wait_send()
 
+        @pl.when(core == 0)
+        def _():
+            lend_copy.wait_send()
+
         @pl.when(core == 1)
         def _():
-            rest_copy.wait_send()
-        route_all(0, 0).wait_send()
+            for copy in (rest_copy, own_copy, lent_copy):
+                copy.wait_send()
 
 
 def solution(mesh):
@@ -323,17 +377,16 @@
             pltpu.VMEM((2, chunks, tokens, CHUNK), f32),
             pltpu.VMEM((chunks, tokens, CHUNK), f32),
             pltpu.VMEM((chunks, tokens, CHUNK), f32),
-            pltpu.VMEM((2, DIRECT, CHUNK), f32),
+            pltpu.VMEM((2 * DIRECT + LENT, CHUNK), f32),
+            pltpu.VMEM((LENT, CHUNK), f32),
+            pltpu.VMEM((LENT, CHUNK), f32),
             pltpu.SemaphoreType.DMA((RING,)),
             pltpu.SemaphoreType.DMA((RING,)),
             pltpu.SemaphoreType.DMA((4,)),
             pltpu.SemaphoreType.DMA,
             pltpu.SemaphoreType.DMA,
-            pltpu.SemaphoreType.DMA,
             pltpu.SemaphoreType.DMA((chunks + 1,)),
-            pltpu.SemaphoreType.DMA,
             pltpu.SemaphoreType.DMA((chunks,)),
-            pltpu.SemaphoreType.DMA,
             pltpu.SemaphoreType.DMA,
             pltpu.SemaphoreType.DMA,
         ]

time: 25.3 us -> 24 us (0.949)
  the two profiles are of different devices: /device:TPU:0 before, /device:TPU:1 now
where the time goes in v3:
time: 24 us; the launch traced here: 23.9 us
  Pallas kernels  23.2 us (97%)
  local copies, waits for them, and re-layouts  0.71 us (3%)
    pallas_call x1, Pallas kernels, local_step(): pl.pallas_call(kernel, out_shape=pltpu.VMEM((tokens, width), bf16), in_sp...  23.2 us
    unnamed x1, local copies, waits for them, and re-layouts  0.71 us

profile of v3, /device:TPU:1, one launch (start us, length us, event | category | flops | bytes accessed | tf_op | source)
XLA Modules:
  0.0 23.9 jit_solution(10831178456180353441)
XLA Ops:
  0.0 23.2 %expert_return.1 = bf16[128,1024]{1,0:T(8,128)(2,1)S(1)} custom-call(bf16[4,8,64,1024]{3,2,1,0:T(8,128)(2,1)} %x_hbm.1, bf16[8,1024,512]{2,1,0:T(8,128)(2,1)} %wg_hbm.1, bf16[8,1024,512]{2,1,0:T(8,128)(2,1)} %wu_hbm.1, bf16[8,512,1024]{2,1,0:T(8,128)(2,1)} %wd_hbm.1, s32[4,8]{1,0:T(4,128)} %fill_hbm.1, s32[8,128]{1,0:T(8,128)} %bitcast.3, s32[8,128]{1,0:T(8,128)} %bitcast.4, ...), custom_call_target="tpu_custom_call" | custom-call | tf_op jit(solution)/shard_map/expert_return/pallas_call | solution.py:394
  23.2 0.7 %copy.10 = bf16[128,1024]{1,0:T(8,128)(2,1)} copy(bf16[128,1024]{1,0:T(8,128)(2,1)S(1)} %expert_return.1) | data formatting | bytes 524288

commit v4 on v3

--- a/solution.py
+++ b/solution.py
@@ -6,8 +6,8 @@
 from jax.sharding import PartitionSpec as P
 
 MESH = pl.DeviceIdType.MESH
-RING = 4
 CHUNK = 256
+EARLY = 3
 DIRECT = 64
 LENT = 32
 BF16_MAX = 3.3895313892515355e38
@@ -24,13 +24,14 @@
 def kernel(x_hbm, wg_hbm, wu_hbm, wd_hbm, fill_hbm, slot_hbm, expert_hbm, gate_hbm, out_ref,
            x_buf, w_buf, wd_buf, fill_buf, id_buf, gate_buf,
            route_out, route_in, mix, hid, rows_buf, sums, from_peer, link_out, link_in, side_in, lent_in, lent_out,
-           w_sem, x_sem, small_sem, send_sem, route_recv, give_recv, link_recv, side_recv, lent_recv):
-    experts = wg_hbm.shape[0]
+           stream_sem, small_sem, send_sem, route_recv, give_recv, link_recv, side_recv, lent_recv):
+    experts, _, ffn = wg_hbm.shape
     capacity, width = x_hbm.shape[2:]
     choices, tokens = slot_hbm.shape
     chunks = width // CHUNK
     pair = 2 * capacity
     half = experts // 2
+    mid = experts - 1 - EARLY
     group = lax.axis_index("dp")
     me = lax.axis_index("ep")
     core = lax.rem(me, 2)
@@ -40,44 +41,54 @@
     far_other = (1 - chip) * 2 + (1 - core)
     sources = (far_other, far, partner, me)
 
-    def start_expert(e):
-        for role in range(2):
-            pltpu.make_async_copy(
-                x_hbm.at[sources[role], e], x_buf.at[e, pl.ds(role * capacity, capacity)],
-                x_sem.at[lax.rem(e, RING)]).start()
+    def start_expert(e, carry):
         for which, src in enumerate((wg_hbm, wu_hbm)):
-            pltpu.make_async_copy(src.at[e], w_buf.at[e, which], w_sem.at[lax.rem(e, RING)]).start()
-
-    def start_step(e, carry):
-        start_expert(e)
+            pltpu.make_async_copy(src.at[e], w_buf.at[e, which], stream_sem.at[e]).start()
         return carry
 
-    def early_down_copy(e):
-        return pltpu.make_async_copy(
-            wd_hbm.at[e, :, pl.ds(0, CHUNK)], wd_buf.at[e, :, pl.ds(0, CHUNK)], x_sem.at[lax.rem(e + half, RING)])
+    def start_late_expert(e, carry):
+        cols = pl.ds(0, CHUNK)
+        pltpu.make_async_copy(wd_hbm.at[e - mid, :, cols], wd_buf.at[e - mid, :, cols], stream_sem.at[e]).start()
+        return start_expert(e, carry)
 
     def wait_expert(e, late):
-        part = x_buf.at[e] if late else x_buf.at[e, pl.ds(0, pair)]
-        pltpu.make_async_copy(part, part, x_sem.at[lax.rem(e, RING)]).wait()
-        pltpu.make_async_copy(w_buf.at[e], w_buf.at[e], w_sem.at[lax.rem(e, RING)]).wait()
+        values = 2 * width * ffn + (ffn * CHUNK if late else 0)
+        part = x_buf.at[:, pl.ds(0, values // (experts * width))]
+        pltpu.make_async_copy(part, part, stream_sem.at[e]).wait()
 
     def down_copy(n):
-        some = pl.ds(half, half) if n == 0 else pl.ds(0, experts)
+        some = pl.ds(EARLY, experts - EARLY) if n == 0 else pl.ds(0, experts)
         cols = pl.ds(n * CHUNK, CHUNK)
-        return pltpu.make_async_copy(
-            wd_hbm.at[some, :, cols], wd_buf.at[some, :, cols], w_sem.at[(experts + n) % RING])
-
-    small = [pltpu.make_async_copy(src, dst, small_sem.at[i]) for i, (src, dst) in enumerate(
-        ((slot_hbm, id_buf.at[0]), (expert_hbm, id_buf.at[1]), (gate_hbm, gate_buf), (fill_hbm, fill_buf)))]
+        return pltpu.make_async_copy(wd_hbm.at[some, :, cols], wd_buf.at[some, :, cols], stream_sem.at[n])
+
+    def start_first_chunk():
+        cols = pl.ds(0, CHUNK)
+        for e in range(EARLY, experts):
+            pltpu.make_async_copy(wd_hbm.at[e, :, cols], wd_buf.at[e, :, cols], stream_sem.at[0]).start()
+
+    small = [pltpu.make_async_copy(src, dst, small_sem.at[i]) for i, src, dst in (
+        (0, slot_hbm, id_buf.at[0]), (0, expert_hbm, id_buf.at[1]), (1, gate_hbm, gate_buf), (2, fill_hbm, fill_buf))]
     for copy in small:
         copy.start()
-    lax.fori_loop(0, RING, start_step, 0)
+    def start_rows(first, count, sem):
+        for role in (first, first + 1):
+            some = pl.ds(0, count) if count < experts else pl.ds(0, experts)
+            pltpu.make_async_copy(
+                x_hbm.at[sources[role], some], x_buf.at[some, pl.ds(role * capacity, capacity)], sem).start()
+
+    start_rows(0, experts, small_sem.at[3])
+    lax.fori_loop(0, half, start_expert, 0)
 
     barrier = pltpu.get_barrier_semaphore()
     for peer in (partner, far, far_other):
         pl.semaphore_signal(barrier, inc=1, device_id=(group, peer), device_id_type=MESH)
 
-    for copy in small:
+    lax.fori_loop(half, mid, start_expert, 0)
+    lax.fori_loop(mid, experts - 1, start_late_expert, 0)
+    start_expert(experts - 1, 0)
+
+    pltpu.make_async_copy(id_buf, id_buf, small_sem.at[0]).wait()
+    for copy in small[2:]:
         copy.wait()
     slot = id_buf[0]
     code = jnp.where(slot >= 0, id_buf[1] * capacity + slot, -1)
@@ -108,12 +119,10 @@
     def first_step(e, carry):
         with jax.named_scope("w_e"):
             wait_expert(e, False)
-
-        @pl.when(e + RING >= half)
-        def _():
-            early_down_copy(e + RING - half).start()
-
-        start_expert(e + RING)
+        @pl.when(e == 0)
+        def _():
+            start_first_chunk()
+
         with jax.named_scope("hid"):
             hidden(0, e)
         return carry
@@ -121,19 +130,8 @@
     def late_step(e, carry):
         with jax.named_scope("w_e"):
             wait_expert(e, True)
-
-        @pl.when(e + RING < experts)
-        def _():
-            early_down_copy(e + RING - half).start()
-            start_expert(e + RING)
-
-        for n in range(RING):
-            @pl.when(e + RING == experts + n)
-            def _():
-                down_copy(n).start()
-
         with jax.named_scope("hid"):
-            rows_of(0, 0, e - half)
+            rows_of(0, 0, e - mid)
             hidden(0, e)
         return carry
 
@@ -192,7 +190,7 @@
         part = pl.ds(skip, tokens - skip)
         return pltpu.make_async_remote_copy(
             src_ref=link_out.at[n, part], dst_ref=link_in.at[n, part], send_sem=send_sem,
-            recv_sem=link_recv.at[n], device_id=(group, far), device_id_type=MESH)
+            recv_sem=link_recv.at[n // (chunks - 1)], device_id=(group, far), device_id_type=MESH)
 
     def send_on(n):
         give_copy(0, n).wait_recv()
@@ -209,28 +207,32 @@
                 (rest_copy, own_copy)[n].start()
         link_copy(n).start()
 
+    remote_rows_in = x_buf.at[:, pl.ds(0, pair)]
+    pltpu.make_async_copy(remote_rows_in, remote_rows_in, small_sem.at[3]).wait()
     lax.fori_loop(0, half, first_step, 0)
     with jax.named_scope("w_route"):
         route_all(0, 0).wait_recv()
     with jax.named_scope("mix"):
         build_mix(0)
-    lax.fori_loop(half, half + 2, late_step, 0)
+    lax.fori_loop(half, mid, first_step, 0)
     with jax.named_scope("mix"):
         build_mix(1)
-    lax.fori_loop(half + 2, experts, late_step, 0)
+    lax.fori_loop(mid, experts - 1, late_step, 0)
+    down_copy(1).start()
+    lax.fori_loop(experts - 1, experts, first_step, 0)
+    for n in range(2, chunks):
+        down_copy(n).start()
 
     def remote_rows(n, between=lambda: None):
         with jax.named_scope("w_d"):
             down_copy(n).wait()
-        if n + RING < chunks:
-            down_copy(n + RING).start()
         with jax.named_scope("rows"):
-            for e in range(half, experts):
+            for e in range(EARLY, experts) if n == 0 else range(half):
                 rows_of(0, n, e)
         between()
         if n > 0:
             with jax.named_scope("rows"):
-                for e in range(half):
+                for e in range(half, experts):
                     rows_of(0, n, e)
 
     def remote_sums(n):
@@ -260,7 +262,7 @@
     remote_rows(0)
     for role in (2, 3):
         pltpu.make_async_copy(
-            x_hbm.at[sources[role]], x_buf.at[:, pl.ds(role * capacity, capacity)], small_sem.at[0]).start()
+            x_hbm.at[sources[role]], x_buf.at[:, pl.ds(role * capacity, capacity)], stream_sem.at[half]).start()
     remote_sums(0)
 
     def send_first():
@@ -284,7 +286,7 @@
             send_on(n - 1)
 
     local_rows = x_buf.at[:, pl.ds(pair, pair)]
-    pltpu.make_async_copy(local_rows, local_rows, small_sem.at[0]).wait()
+    pltpu.make_async_copy(local_rows, local_rows, stream_sem.at[half]).wait()
 
     def local_step(e, carry):
         hidden(2, e)
@@ -329,7 +331,14 @@
     for n in range(chunks):
         near = sums[1, 1, n] + from_peer[1, n]
         with jax.named_scope("fin_link"):
-            link_copy(n).wait_recv()
+            if n == 0:
+                count = ((chunks - 1) * tokens - DIRECT - LENT) // chunks
+                part = link_in.at[:, pl.ds(0, count)]
+                pltpu.make_async_remote_copy(
+                    src_ref=part, dst_ref=part, send_sem=send_sem, recv_sem=link_recv.at[0],
+                    device_id=(group, far), device_id_type=MESH).wait_recv()
+            if n == chunks - 1:
+                link_copy(n).wait_recv()
         out_ref[:, pl.ds(n * CHUNK, CHUNK)] = (near + link_in[n]).astype(jnp.bfloat16)
 
     with jax.named_scope("w_send"):
@@ -380,13 +389,12 @@
             pltpu.VMEM((2 * DIRECT + LENT, CHUNK), f32),
             pltpu.VMEM((LENT, CHUNK), f32),
             pltpu.VMEM((LENT, CHUNK), f32),
-            pltpu.SemaphoreType.DMA((RING,)),
-            pltpu.SemaphoreType.DMA((RING,)),
+            pltpu.SemaphoreType.DMA((experts,)),
             pltpu.SemaphoreType.DMA((4,)),
             pltpu.SemaphoreType.DMA,
             pltpu.SemaphoreType.DMA,
             pltpu.SemaphoreType.DMA((chunks + 1,)),
-            pltpu.SemaphoreType.DMA((chunks,)),
+            pltpu.SemaphoreType.DMA((2,)),
             pltpu.SemaphoreType.DMA,
             pltpu.SemaphoreType.DMA,
         ]

time: 24 us -> 23.9 us (level)
  no operation moved by 1% of the time
where the time goes in v4:
time: 23.9 us; the launch traced here: 23.8 us
  Pallas kernels  23.1 us (97%)
  local copies, waits for them, and re-layouts  0.71 us (3%)
    pallas_call x1, Pallas kernels, local_step(): pl.pallas_call(kernel, out_shape=pltpu.VMEM((tokens, width), bf16), in_sp...  23.1 us
    unnamed x1, local copies, waits for them, and re-layouts  0.71 us

profile of v4, /device:TPU:1, one launch (start us, length us, event | category | flops | bytes accessed | tf_op | source)
XLA Modules:
  0.0 23.8 jit_solution(12947114484883069476)
XLA Ops:
  0.0 23.1 %expert_return.1 = bf16[128,1024]{1,0:T(8,128)(2,1)S(1)} custom-call(bf16[4,8,64,1024]{3,2,1,0:T(8,128)(2,1)} %x_hbm.1, bf16[8,1024,512]{2,1,0:T(8,128)(2,1)} %wg_hbm.1, bf16[8,1024,512]{2,1,0:T(8,128)(2,1)} %wu_hbm.1, bf16[8,512,1024]{2,1,0:T(8,128)(2,1)} %wd_hbm.1, s32[4,8]{1,0:T(4,128)} %fill_hbm.1, s32[8,128]{1,0:T(8,128)} %bitcast.3, s32[8,128]{1,0:T(8,128)} %bitcast.4, ...), custom_call_target="tpu_custom_call" | custom-call | tf_op jit(solution)/shard_map/expert_return/pallas_call | solution.py:402
  23.1 0.7 %copy.10 = bf16[128,1024]{1,0:T(8,128)(2,1)} copy(bf16[128,1024]{1,0:T(8,128)(2,1)S(1)} %expert_return.1) | data formatting | bytes 524288

commit v5 on v4

--- a/solution.py
+++ b/solution.py
@@ -9,7 +9,8 @@
 CHUNK = 256
 EARLY = 3
 DIRECT = 64
-LENT = 32
+LENT = 64
+AWAY = 80
 BF16_MAX = 3.3895313892515355e38
 
 
@@ -24,7 +25,9 @@
 def kernel(x_hbm, wg_hbm, wu_hbm, wd_hbm, fill_hbm, slot_hbm, expert_hbm, gate_hbm, out_ref,
            x_buf, w_buf, wd_buf, fill_buf, id_buf, gate_buf,
            route_out, route_in, mix, hid, rows_buf, sums, from_peer, link_out, link_in, side_in, lent_in, lent_out,
-           stream_sem, small_sem, send_sem, route_recv, give_recv, link_recv, side_recv, lent_recv):
+           away_out, away_in, final_out, final_in,
+           stream_sem, small_sem, send_sem, route_recv, give_recv, link_recv, side_recv, lent_recv,
+           away_recv):
     experts, _, ffn = wg_hbm.shape
     capacity, width = x_hbm.shape[2:]
     choices, tokens = slot_hbm.shape
@@ -167,7 +170,7 @@
     def give_copy(kind, n):
         return pltpu.make_async_remote_copy(
             src_ref=sums.at[kind, 0, n], dst_ref=from_peer.at[kind, n], send_sem=send_sem,
-            recv_sem=give_recv.at[n if kind == 0 else chunks], device_id=(group, partner), device_id_type=MESH)
+            recv_sem=give_recv.at[n if kind == 0 else chunks + (n == chunks - 1)], device_id=(group, partner), device_id_type=MESH)
 
     direct_copy = pltpu.make_async_remote_copy(
         src_ref=sums.at[0, 1 - core, 0, pl.ds(0, DIRECT)], dst_ref=side_in.at[pl.ds(core * DIRECT, DIRECT)],
@@ -185,12 +188,28 @@
         src_ref=link_out.at[1, pl.ds(0, LENT)], dst_ref=link_in.at[1, pl.ds(0, LENT)], send_sem=send_sem,
         recv_sem=side_recv, device_id=(group, far), device_id_type=MESH)
 
+    lends_last = (chip == 0) & (core == 1)
+    adds_last = (chip == 1) & (core == 1)
+    away_copy = pltpu.make_async_remote_copy(
+        src_ref=away_out, dst_ref=away_in, send_sem=send_sem, recv_sem=away_recv,
+        device_id=(group, far), device_id_type=MESH)
+    final_copy = pltpu.make_async_remote_copy(
+        src_ref=final_out, dst_ref=final_in, send_sem=send_sem, recv_sem=away_recv,
+        device_id=(group, far), device_id_type=MESH)
+
+    def last_copy(skip):
+        part = pl.ds(skip, tokens - skip)
+        n = chunks - 1
+        return pltpu.make_async_remote_copy(
+            src_ref=link_out.at[n, part], dst_ref=link_in.at[n, part], send_sem=send_sem,
+            recv_sem=link_recv.at[1], device_id=(group, far), device_id_type=MESH)
+
     def link_copy(n):
         skip = DIRECT if n == 0 else LENT if n == 1 else 0
         part = pl.ds(skip, tokens - skip)
         return pltpu.make_async_remote_copy(
             src_ref=link_out.at[n, part], dst_ref=link_in.at[n, part], send_sem=send_sem,
-            recv_sem=link_recv.at[n // (chunks - 1)], device_id=(group, far), device_id_type=MESH)
+            recv_sem=link_recv.at[0], device_id=(group, far), device_id_type=MESH)
 
     def send_on(n):
         give_copy(0, n).wait_recv()
@@ -205,7 +224,16 @@
             @pl.when(core == 1)
             def _():
                 (rest_copy, own_copy)[n].start()
-        link_copy(n).start()
+        if n < chunks - 1:
+            link_copy(n).start()
+        else:
+            @pl.when(adds_last)
+            def _():
+                last_copy(AWAY).start()
+
+            @pl.when(jnp.logical_not(adds_last))
+            def _():
+                last_copy(0).start()
 
     remote_rows_in = x_buf.at[:, pl.ds(0, pair)]
     pltpu.make_async_copy(remote_rows_in, remote_rows_in, small_sem.at[3]).wait()
@@ -224,8 +252,9 @@
         down_copy(n).start()
 
     def remote_rows(n, between=lambda: None):
-        with jax.named_scope("w_d"):
-            down_copy(n).wait()
+        if n < chunks - 1:
+            with jax.named_scope("w_d"):
+                down_copy(n).wait()
         with jax.named_scope("rows"):
             for e in range(EARLY, experts) if n == 0 else range(half):
                 rows_of(0, n, e)
@@ -279,12 +308,26 @@
         with jax.named_scope("send_on"):
             send_on(0)
 
-    for n in range(2, chunks):
+    last = chunks - 1
+    last = chunks - 1
+
+    def last_remote_chunk():
+        remote_rows(last)
+        remote_sums(last)
+
+    for n in range(2, last):
         remote_rows(n)
         remote_sums(n)
         with jax.named_scope("send_on"):
             send_on(n - 1)
 
+    down_copy(last).wait()
+    @pl.when(chip == 1)
+    def _():
+        last_remote_chunk()
+        with jax.named_scope("send_on"):
+            send_on(last - 1)
+
     local_rows = x_buf.at[:, pl.ds(pair, pair)]
     pltpu.make_async_copy(local_rows, local_rows, stream_sem.at[half]).wait()
 
@@ -292,13 +335,7 @@
         hidden(2, e)
         return carry
 
-    lax.fori_loop(0, 2, local_step, 0)
-    send_on(chunks - 1)
-    with jax.named_scope("phase1L"):
-        lax.fori_loop(2, experts, local_step, 0)
-    for role in (2, 3):
-        build_mix(role)
-    for n in range(chunks):
+    def local_chunk(n):
         with jax.named_scope("rows2"):
             for e in range(experts):
                 rows_of(2, n, e)
@@ -307,9 +344,59 @@
             sums[1, 1, n] = mixed(3)
             give_copy(1, n).start()
 
+    lax.fori_loop(0, 3, local_step, 0)
+    with jax.named_scope("send_on"):
+        @pl.when(chip == 0)
+        def _():
+            send_on(last - 1)
+
+        @pl.when(chip == 1)
+        def _():
+            send_on(last)
+    with jax.named_scope("phase1L"):
+        lax.fori_loop(3, experts, local_step, 0)
+    for role in (2, 3):
+        build_mix(role)
+    local_chunk(last)
+
+    @pl.when(chip == 0)
+    def _():
+        last_remote_chunk()
+
+    with jax.named_scope("away"):
+        @pl.when(lends_last)
+        def _():
+            give_copy(1, last).wait_recv()
+            away_out[...] = sums[1, 1, last, 0:AWAY] + from_peer[1, last, 0:AWAY]
+            away_copy.start()
+
+    local_chunk(0)
+
+    @pl.when(chip == 0)
+    def _():
+        with jax.named_scope("send_on"):
+            send_on(last)
+
+    for n in range(1, last - 1):
+        local_chunk(n)
+
+    with jax.named_scope("away_add"):
+        @pl.when(adds_last)
+        def _():
+            away_copy.wait_recv()
+            final_out[...] = (away_in[...] + link_out[last, 0:AWAY]).astype(jnp.bfloat16)
+            final_copy.start()
+
+    local_chunk(last - 1)
+
+    @pl.when(jnp.logical_not(lends_last))
+    def _():
+        give_copy(1, last).wait_recv()
+
     with jax.named_scope("fin_give"):
+        given = from_peer.at[1, pl.ds(0, last)]
         pltpu.make_async_remote_copy(
-            src_ref=sums.at[1, 0], dst_ref=from_peer.at[1], send_sem=send_sem, recv_sem=give_recv.at[chunks],
+            src_ref=given, dst_ref=given, send_sem=send_sem, recv_sem=give_recv.at[chunks],
             device_id=(group, partner), device_id_type=MESH).wait_recv()
 
     with jax.named_scope("fin_side"):
@@ -337,9 +424,23 @@
                 pltpu.make_async_remote_copy(
                     src_ref=part, dst_ref=part, send_sem=send_sem, recv_sem=link_recv.at[0],
                     device_id=(group, far), device_id_type=MESH).wait_recv()
-            if n == chunks - 1:
-                link_copy(n).wait_recv()
-        out_ref[:, pl.ds(n * CHUNK, CHUNK)] = (near + link_in[n]).astype(jnp.bfloat16)
+        if n < last:
+            out_ref[:, pl.ds(n * CHUNK, CHUNK)] = (near + link_in[n]).astype(jnp.bfloat16)
+    cols = pl.ds(last * CHUNK, CHUNK)
+
+    @pl.when(lends_last)
+    def _():
+        final_copy.wait_recv()
+        out_ref[0:AWAY, cols] = final_in[...]
+        with jax.named_scope("fin_last"):
+            last_copy(AWAY).wait_recv()
+        out_ref[AWAY:, cols] = (near[AWAY:] + link_in[last, AWAY:]).astype(jnp.bfloat16)
+
+    @pl.when(jnp.logical_not(lends_last))
+    def _():
+        with jax.named_scope("fin_last"):
+            last_copy(0).wait_recv()
+        out_ref[:, cols] = (near + link_in[last]).astype(jnp.bfloat16)
 
     with jax.named_scope("w_send"):
         def wait_sent(ref):
@@ -349,8 +450,20 @@
 
         wait_sent(route_in)
         wait_sent(from_peer)
-        for n in range(chunks):
+        for n in range(last):
             link_copy(n).wait_send()
+        @pl.when(lends_last)
+        def _():
+            away_copy.wait_send()
+
+        @pl.when(adds_last)
+        def _():
+            last_copy(AWAY).wait_send()
+            final_copy.wait_send()
+
+        @pl.when(jnp.logical_not(adds_last))
+        def _():
+            last_copy(0).wait_send()
         direct_copy.wait_send()
 
         @pl.when(core == 0)
@@ -389,12 +502,17 @@
             pltpu.VMEM((2 * DIRECT + LENT, CHUNK), f32),
             pltpu.VMEM((LENT, CHUNK), f32),
             pltpu.VMEM((LENT, CHUNK), f32),
+            pltpu.VMEM((AWAY, CHUNK), f32),
+            pltpu.VMEM((AWAY, CHUNK), f32),
+            pltpu.VMEM((AWAY, CHUNK), bf16),
+            pltpu.VMEM((AWAY, CHUNK), bf16),
             pltpu.SemaphoreType.DMA((experts,)),
             pltpu.SemaphoreType.DMA((4,)),
             pltpu.SemaphoreType.DMA,
             pltpu.SemaphoreType.DMA,
-            pltpu.SemaphoreType.DMA((chunks + 1,)),
+            pltpu.SemaphoreType.DMA((chunks + 2,)),
             pltpu.SemaphoreType.DMA((2,)),
+            pltpu.SemaphoreType.DMA,
             pltpu.SemaphoreType.DMA,
             pltpu.SemaphoreType.DMA,
         ]

time: 23.9 us -> 23.5 us (0.983)
  Pallas kernels: 23.1 us -> 22.7 us
    pallas_call x1, Pallas kernels: 23.1 us -> 22.7 us  [local_step(): pl.pallas_call(kernel, out_shape=pltpu.VMEM((tokens, width), bf16), in_sp...]
where the time goes in v5:
time: 23.5 us; the launch traced here: 23.4 us
  Pallas kernels  22.7 us (97%)
  local copies, waits for them, and re-layouts  0.71 us (3%)
    pallas_call x1, Pallas kernels, local_step(): pl.pallas_call(kernel, out_shape=pltpu.VMEM((tokens, width), bf16), in_sp...  22.7 us
    unnamed x1, local copies, waits for them, and re-layouts  0.71 us

profile of v5, /device:TPU:1, one launch (start us, length us, event | category | flops | bytes accessed | tf_op | source)
XLA Modules:
  0.0 23.4 jit_solution(502796960057453946)
XLA Ops:
  0.0 22.7 %expert_return.1 = bf16[128,1024]{1,0:T(8,128)(2,1)S(1)} custom-call(bf16[4,8,64,1024]{3,2,1,0:T(8,128)(2,1)} %x_hbm.1, bf16[8,1024,512]{2,1,0:T(8,128)(2,1)} %wg_hbm.1, bf16[8,1024,512]{2,1,0:T(8,128)(2,1)} %wu_hbm.1, bf16[8,512,1024]{2,1,0:T(8,128)(2,1)} %wd_hbm.1, s32[4,8]{1,0:T(4,128)} %fill_hbm.1, s32[8,128]{1,0:T(8,128)} %bitcast.3, s32[8,128]{1,0:T(8,128)} %bitcast.4, ...), custom_call_target="tpu_custom_call" | custom-call | tf_op jit(solution)/shard_map/expert_return/pallas_call | solution.py:520
  22.7 0.7 %copy.10 = bf16[128,1024]{1,0:T(8,128)(2,1)} copy(bf16[128,1024]{1,0:T(8,128)(2,1)S(1)} %expert_return.1) | data formatting | bytes 524288
